TPU v7x, 32 devices: a whole 2x2x4 slice. The times are simulated.
32 devices in a mesh: grp: 2 (over x), trn: 8 (over z, y), tst: 2 (over core).
Axes of the slice: x: 2, y: 2, z: 4, core: 2. Of those that a mesh axis runs over, the one named last changes fastest.
Arguments:
- test_points: bfloat16 [64, 8192], P(None, ('grp', 'tst')), parts along dimension 1, may hold values from -9 to 9
- train_points: bfloat16 [64, 65536], P(None, ('grp', 'trn')), parts along dimension 1, may hold values from -6 to 6
- weights: bfloat16 [65536], P(('grp', 'trn')), parts along dimension 0, may hold values from -6 to 6
- factor: bfloat16 [65536, 512], P(('grp', 'trn')), parts along dimension 0, may hold values from -1.14904852 to 1.14904852
Outputs:
- mean: float32 [8192], P(('grp', 'tst')), parts along dimension 0
- variance: float32 [8192], P(('grp', 'tst')), parts along dimension 0
There are 2 independent parts, one for each index of `grp`. A program takes and returns all parts, laid end to end along the dimension named above; each array names one. Nothing has to cross between parts.
All inputs are finite; a program needn't handle non-finite values.
Results may differ from a plain program's by a relative error of at most 0.0033.
Values sent between devices are 32-bit elements; how exact they have to be, the bound alone decides.
A program may use at most 64 MiB of HBM per device.

v0:
```python
import math

import jax
import jax.numpy as jnp
from jax import lax
from jax.sharding import PartitionSpec as P


def on_device(test_points, train_points, weights, factor):
    rows = test_points.shape[1]
    local = train_points.shape[1]
    dim = test_points.shape[0]
    width = factor.shape[1]
    test_sq = jnp.sum(test_points.astype(jnp.float32) ** 2, axis=0)
    block = math.gcd(local, 1024)
    turns = local // block

    def step(index, carry):
        mean_acc, proj_acc = carry
        start = (index * block).astype(jnp.int32)
        points = lax.dynamic_slice_in_dim(train_points, start, block, 1)
        wblock = lax.dynamic_slice_in_dim(weights, start, block, 0)
        fblock = lax.dynamic_slice_in_dim(factor, start, block, 0)
        train_sq = jnp.sum(points.astype(jnp.float32) ** 2, axis=0)
        cross = lax.dot_general(
            test_points, points, (((0,), (0,)), ((), ())), preferred_element_type=jnp.float32
        )
        kernel = jnp.exp(
            -(test_sq[:, None] + train_sq[None, :] - 2.0 * cross) * (4.0 / dim)
        ).astype(jnp.bfloat16)
        mean_acc = mean_acc + jnp.dot(kernel, wblock, preferred_element_type=jnp.float32)
        proj_acc = proj_acc + jnp.dot(kernel, fblock, preferred_element_type=jnp.float32)
        return (mean_acc, proj_acc)

    init = (jnp.zeros((rows,), jnp.float32), jnp.zeros((rows, width), jnp.float32))
    mean_part, proj_part = lax.fori_loop(0, turns, step, init)
    mean_share, proj_share = (
        lax.psum_scatter(mean_part, "trn", scatter_dimension=0, tiled=True),
        lax.psum_scatter(proj_part, "trn", scatter_dimension=0, tiled=True),
    )
    var_share = 1.0 - jnp.sum(proj_share * proj_share, axis=1)
    mean, variance = (
        lax.all_gather(mean_share, "trn", axis=0, tiled=True),
        lax.all_gather(var_share, "trn", axis=0, tiled=True),
    )
    return (mean, variance)


def solution(mesh):
    in_specs = (
        P(None, ("grp", "tst")),
        P(None, ("grp", "trn")),
        P(("grp", "trn")),
        P(("grp", "trn"), None),
    )
    out_specs = (P(("grp", "tst")), P(("grp", "tst")))
    return jax.shard_map(
        on_device, mesh=mesh, in_specs=in_specs, out_specs=out_specs, check_vma=False
    )
```

profile of v0, /device:TPU:0, one launch (start us, length us, event | category | flops | bytes accessed | tf_op | source)
XLA Modules:
  0.0 189.9 jit_solution(13181331703198562564)
XLA Ops:
  7.2 1.0 multiply_reduce_fusion.2
  8.2 61.1 %while.16 = (s32[]{:T(128)}, f32[2048]{0:T(1024)S(1)}, f32[2048,512]{1,0:T(8,128)}, f32[2048]{0:T(1024)S(1)}, bf16[64,4096]{1,0:T(8,128)(2,1)}, /*index=5*/bf16[...) while((s32[]{:T(128)}, f32[2048]{0:T(1024)S(1)}, ...), condition=%wide.region_3.0_spmd.clone, body=%wide.region_1.0_spmd.clone.sunk | while | flops 2434993152 | bytes 39381208 | solution.py:36
  8.3 0.9 multiply_reduce_fusion.4
  9.2 5.0 %fusion.27 = bf16[2048,1024]{0,1:T(8,128)(2,1)} fusion(bf16[64,2048]{1,0:T(8,128)(2,1)} %get-tuple-element.265, f32[1024]{0:T(1024)S(1)} %multiply_reduce_fusion.4, f32[2048]{0:T(1024)S(1)} %get-tuple-element.263, bf16[64,4096]{1,0:T(8,128)(2,1)} %get-tuple-element.264, s32[]{:T(128)S(6)} %select_n.11), kind=kOutput, calls=%fused_computation.4.clone.1 | convolution fusion | flops 281018368 | bytes 4599812 | tf_op jit(solution)/shard_map/while/body/eval_jaxpr/dot_general | solution.py:25
  14.2 7.0 %select_add_fusion.5 = f32[2048,512]{1,0:T(8,128)} fusion(f32[2048,512]{1,0:T(8,128)} %get-tuple-element.250, bf16[2048,1024]{0,1:T(8,128)(2,1)} %fusion.27, pred[]{:T(512)S(6)} %compare.3, bf16[4096,512]{1,0:T(8,128)(2,1)} %get-tuple-element.267, s32[]{:T(128)S(6)} %select_n.11), kind=kOutput, calls=%fused_computation.5.clone.1 | convolution fusion | flops 2149580800 | bytes 13631493 | tf_op jit(solution)/shard_map/while/body/eval_jaxpr/dot_general | solution.py:32
  21.2 0.7 dynamic_slice.36
  21.9 0.7 fusion.28
  22.6 0.9 multiply_reduce_fusion.4
  23.5 5.0 %fusion.27 = bf16[2048,1024]{0,1:T(8,128)(2,1)} fusion(bf16[64,2048]{1,0:T(8,128)(2,1)} %get-tuple-element.265, f32[1024]{0:T(1024)S(1)} %multiply_reduce_fusion.4, f32[2048]{0:T(1024)S(1)} %get-tuple-element.263, bf16[64,4096]{1,0:T(8,128)(2,1)} %get-tuple-element.264, s32[]{:T(128)S(6)} %select_n.11), kind=kOutput, calls=%fused_computation.4.clone.1 | convolution fusion | flops 281018368 | bytes 4599812 | tf_op jit(solution)/shard_map/while/body/eval_jaxpr/dot_general | solution.py:25
  28.5 8.3 %select_add_fusion.5 = f32[2048,512]{1,0:T(8,128)} fusion(f32[2048,512]{1,0:T(8,128)} %get-tuple-element.250, bf16[2048,1024]{0,1:T(8,128)(2,1)} %fusion.27, pred[]{:T(512)S(6)} %compare.3, bf16[4096,512]{1,0:T(8,128)(2,1)} %get-tuple-element.267, s32[]{:T(128)S(6)} %select_n.11), kind=kOutput, calls=%fused_computation.5.clone.1 | convolution fusion | flops 2149580800 | bytes 13631493 | tf_op jit(solution)/shard_map/while/body/eval_jaxpr/dot_general | solution.py:32
  36.8 0.7 dynamic_slice.36
  37.5 0.7 fusion.28
  38.2 0.9 multiply_reduce_fusion.4
  39.1 5.0 %fusion.27 = bf16[2048,1024]{0,1:T(8,128)(2,1)} fusion(bf16[64,2048]{1,0:T(8,128)(2,1)} %get-tuple-element.265, f32[1024]{0:T(1024)S(1)} %multiply_reduce_fusion.4, f32[2048]{0:T(1024)S(1)} %get-tuple-element.263, bf16[64,4096]{1,0:T(8,128)(2,1)} %get-tuple-element.264, s32[]{:T(128)S(6)} %select_n.11), kind=kOutput, calls=%fused_computation.4.clone.1 | convolution fusion | flops 281018368 | bytes 4599812 | tf_op jit(solution)/shard_map/while/body/eval_jaxpr/dot_general | solution.py:25
  44.1 8.3 %select_add_fusion.5 = f32[2048,512]{1,0:T(8,128)} fusion(f32[2048,512]{1,0:T(8,128)} %get-tuple-element.250, bf16[2048,1024]{0,1:T(8,128)(2,1)} %fusion.27, pred[]{:T(512)S(6)} %compare.3, bf16[4096,512]{1,0:T(8,128)(2,1)} %get-tuple-element.267, s32[]{:T(128)S(6)} %select_n.11), kind=kOutput, calls=%fused_computation.5.clone.1 | convolution fusion | flops 2149580800 | bytes 13631493 | tf_op jit(solution)/shard_map/while/body/eval_jaxpr/dot_general | solution.py:32
  52.4 0.7 dynamic_slice.36
  53.1 0.7 fusion.28
  53.7 0.9 multiply_reduce_fusion.4
  54.7 5.0 %fusion.27 = bf16[2048,1024]{0,1:T(8,128)(2,1)} fusion(bf16[64,2048]{1,0:T(8,128)(2,1)} %get-tuple-element.265, f32[1024]{0:T(1024)S(1)} %multiply_reduce_fusion.4, f32[2048]{0:T(1024)S(1)} %get-tuple-element.263, bf16[64,4096]{1,0:T(8,128)(2,1)} %get-tuple-element.264, s32[]{:T(128)S(6)} %select_n.11), kind=kOutput, calls=%fused_computation.4.clone.1 | convolution fusion | flops 281018368 | bytes 4599812 | tf_op jit(solution)/shard_map/while/body/eval_jaxpr/dot_general | solution.py:25
  59.7 8.3 %select_add_fusion.5 = f32[2048,512]{1,0:T(8,128)} fusion(f32[2048,512]{1,0:T(8,128)} %get-tuple-element.250, bf16[2048,1024]{0,1:T(8,128)(2,1)} %fusion.27, pred[]{:T(512)S(6)} %compare.3, bf16[4096,512]{1,0:T(8,128)(2,1)} %get-tuple-element.267, s32[]{:T(128)S(6)} %select_n.11), kind=kOutput, calls=%fused_computation.5.clone.1 | convolution fusion | flops 2149580800 | bytes 13631493 | tf_op jit(solution)/shard_map/while/body/eval_jaxpr/dot_general | solution.py:32
  68.0 0.7 dynamic_slice.36
  68.7 0.7 fusion.28
  69.4 0.6 copy-done.1
  70.0 0.6 dynamic-slice
  71.2 24.6 %all-reduce = f32[2048]{0:T(1024)S(1)} all-reduce(f32[2048]{0:T(1024)S(1)} %get-tuple-element.142), channel_id=2, replica_groups=mesh['grp'=2,'trn'=8,'tst'=2] {'trn'}, use_global_device_ids=true, to_apply=%region_4.0.clone | all-reduce | flops 2048 | bytes 16384
  95.8 0.1 dynamic-slice.1
  95.9 17.1 %all-gather = f32[8,1,256]{2,1,0:T(1,128)S(1)} all-gather(f32[1,1,256]{2,1,0:T(1,128)S(1)} %bitcast.35), channel_id=1, replica_groups=mesh['grp'=2,'trn'=8,'tst'=2] {'trn'}, dimensions={0}, use_global_device_ids=true | all-gather | bytes 9216 | tf_op jit(solution)/shard_map/all_gather | solution.py:43
  112.9 48.5 %reduce-scatter.2.cloned.1.call-done = f32[256,512]{1,0:T(8,128)} async-done(((f32[2048,512]{1,0:T(8,128)}), f32[256,512]{1,0:T(8,128)}) %reduce-scatter.2.cloned.1.call-update) | async-done | bytes 524304 | tf_op jit(solution)/shard_map/reduce_scatter | solution.py:39
  161.4 1.2 multiply_reduce_fusion.1
  162.6 19.2 %all-gather.1 = f32[8,1,256]{2,1,0:T(1,128)S(1)} all-gather(f32[1,1,256]{2,1,0:T(1,128)S(1)} %bitcast.36), channel_id=1, replica_groups=mesh['grp'=2,'trn'=8,'tst'=2] {'trn'}, dimensions={0}, use_global_device_ids=true | all-gather | bytes 9216 | tf_op jit(solution)/shard_map/all_gather | solution.py:44
  181.8 0.6 copy.17
  182.4 0.6 copy.18
  (22 shorter events, 0.1 us)
Async XLA Ops:
  7.2 154.3 %reduce-scatter.2.cloned.1.call-start = ((), (), s32[]{:S(2)}) async-start(), calls=%async_computation.1 | async-start | bytes 4718592 | tf_op jit(solution)/shard_map/reduce_scatter | solution.py:39
  14.2 7.7 %copy-start = (bf16[2048,1024]{0,1:T(8,128)(2,1)S(1)}, bf16[2048,1024]{0,1:T(8,128)(2,1)}, u32[]{:S(2)}) copy-start(bf16[2048,1024]{0,1:T(8,128)(2,1)} %fusion.27) | copy-start | bytes 12582916 | tf_op jit(solution)/shard_map/while
  28.5 9.0 %copy-start = (bf16[2048,1024]{0,1:T(8,128)(2,1)S(1)}, bf16[2048,1024]{0,1:T(8,128)(2,1)}, u32[]{:S(2)}) copy-start(bf16[2048,1024]{0,1:T(8,128)(2,1)} %fusion.27) | copy-start | bytes 12582916 | tf_op jit(solution)/shard_map/while
  44.1 9.0 %copy-start = (bf16[2048,1024]{0,1:T(8,128)(2,1)S(1)}, bf16[2048,1024]{0,1:T(8,128)(2,1)}, u32[]{:S(2)}) copy-start(bf16[2048,1024]{0,1:T(8,128)(2,1)} %fusion.27) | copy-start | bytes 12582916 | tf_op jit(solution)/shard_map/while
  59.7 9.0 %copy-start = (bf16[2048,1024]{0,1:T(8,128)(2,1)S(1)}, bf16[2048,1024]{0,1:T(8,128)(2,1)}, u32[]{:S(2)}) copy-start(bf16[2048,1024]{0,1:T(8,128)(2,1)} %fusion.27) | copy-start | bytes 12582916 | tf_op jit(solution)/shard_map/while
  69.3 0.7 copy-start.1
Sparse Core Ops, SparseCore 0:
  69.5 91.9 reduce-scatter.1
where the time goes:
time: 190 us
  blocking collectives  60.9 us (32%)
  matrix products  54.4 us (29%)
  waiting for transfers between devices  48.5 us (26%)
  between operations  14.7 us (8%)
  other arithmetic  6.01 us (3%)
  local copies, waits for them, and re-layouts  5.26 us (3%)
    reduce_scatter x1, waiting for transfers between devices, on_device(): lax.psum_scatter(proj_part, 'trn', scatter_dimension=0, tiled=True)  48.5 us
    dot_general x4, matrix products, step(): jnp.dot(kernel, fblock, preferred_element_type=jnp.float32)  31.8 us
    unnamed x1, blocking collectives  24.6 us
    dot_general x4, matrix products, step(): lax.dot_general(test_points, points, (((0,), (0,)), ((), ())), preferred_...  20 us
    all_gather x1, blocking collectives, on_device(): lax.all_gather(var_share, 'trn', axis=0, tiled=True)  19.2 us
    all_gather x1, blocking collectives, on_device(): lax.all_gather(mean_share, 'trn', axis=0, tiled=True)  17.1 us
  transfers between devices with their start and end apart: 1, of which 1 were waited for; matrix products, arithmetic and copies ran while one was open for 0% of the time, Pallas kernels for 0%

commit v1 on v0

--- a/solution.py
+++ b/solution.py
@@ -1,9 +1,377 @@
+import functools
 import math
 
 import jax
 import jax.numpy as jnp
 from jax import lax
+from jax.experimental import pallas as pl
+from jax.experimental.pallas import tpu as pltpu
 from jax.sharding import PartitionSpec as P
+
+LOG2E = 1.4426950408889634
+STEPS = 8
+CHUNK = 1024
+LINE = 4
+LAG_Y = 3
+LAG_B = (0, 3, 5, 7)
+LAG_A = (0, 5, 7, 9)
+LAG_X = 10
+
+
+def pieces(value):
+    high = value.astype(jnp.bfloat16).astype(jnp.float32)
+    rest = value - high
+    middle = rest.astype(jnp.bfloat16).astype(jnp.float32)
+    low = (rest - middle).astype(jnp.bfloat16).astype(jnp.float32)
+    return high, middle, low
+
+
+def pick(row, table, default):
+    value = default
+    for index, entry in table:
+        value = jnp.where(row == index, entry, value)
+    return value
+
+
+def kernel(
+    test_ref, train_ref, weights_ref, factor_ref, mean_ref, var_ref,
+    test_aug, train_aug, wide, part, got_y, got_br, got_bl, got_ar, got_al, got_x,
+    mean_acc, var_acc, mean_box, var_box,
+    s_y, r_y, s_br, r_br, s_bl, r_bl, s_ar, r_ar, s_al, r_al, s_x, r_x,
+    s_mean, r_mean, s_var, r_var,
+):
+    count = mean_box.shape[0]
+    pair = count // LINE
+    last = LINE - 1
+    me = lax.axis_index("trn")
+    z = me // pair
+    y = me % pair
+    dim, rows = test_ref.shape
+    local = train_ref.shape[1]
+    depth = test_aug.shape[1]
+    group = rows // (8 * STEPS)
+    span = rows // 4
+    other = z * pair + (1 - y)
+    up, down = me + pair, me - pair
+
+    barrier = pltpu.get_barrier_semaphore()
+
+    def greet(k, carry):
+        pl.semaphore_signal(barrier, inc=1, device_id={"trn": lax.rem(me + k, count)})
+        return carry
+
+    lax.fori_loop(1, count, greet, 0)
+
+    def prepare_train(index, carry):
+        cols = pl.ds(pl.multiple_of(index * 512, 512), 512)
+        points = train_ref[:, cols]
+        squares = points.astype(jnp.float32) ** 2
+        norm = jnp.sum(squares, axis=0, keepdims=True) * (-4.0 / dim)
+        high, middle, low = pieces(norm)
+        row = lax.broadcasted_iota(jnp.int32, (16, 512), 0)
+        one = jnp.float32(1.0)
+        extra = pick(row, ((0, one), (1, one), (2, one), (3, high), (4, middle), (5, low)), jnp.float32(0.0))
+        train_aug[:dim, cols] = points
+        train_aug[dim : dim + 16, cols] = extra.astype(jnp.bfloat16)
+        train_aug[dim + 16 :, cols] = jnp.zeros((depth - dim - 16, 512), jnp.bfloat16)
+        return carry
+
+    lax.fori_loop(0, local // 512, prepare_train, 0)
+    wide[...] = weights_ref[...].astype(jnp.float32)
+
+    def prepare_test(index, carry):
+        cols = pl.ds(pl.multiple_of(index * 256, 256), 256)
+        points = test_ref[:, cols].astype(jnp.float32)
+        norm = jnp.sum(points * points, axis=0, keepdims=True) * (-4.0 / dim)
+        high, middle, low = pieces(norm)
+        row = lax.broadcasted_iota(jnp.int32, (8, 256), 0)
+        one = jnp.float32(1.0)
+        extra = pick(row, ((0, high), (1, middle), (2, low), (3, one), (4, one), (5, one)), jnp.float32(0.0))
+        whole = jnp.concatenate(
+            [points * (8.0 / dim), extra, jnp.zeros((depth - dim - 8, 256), jnp.float32)], axis=0
+        )
+        test_aug[cols, :] = whole.T.astype(jnp.bfloat16)
+        return carry
+
+    lax.fori_loop(0, rows // 256, prepare_test, 0)
+
+    def row_of(owner, kind, step):
+        return pl.multiple_of(owner * span + kind * (span // 2) + step * group, group)
+
+    def places(step):
+        return (
+            row_of(2, 0, step), row_of(3, 0, step), row_of(0, 0, step), row_of(1, 0, step),
+            row_of(1 - y, 1, step), row_of(3 - y, 1, step), row_of(y, 1, step), row_of(2 + y, 1, step),
+        )
+
+    def compute(step):
+        where = places(step)
+        left = jnp.concatenate([test_aug[pl.ds(at, group), :] for at in where], axis=0)
+        total = None
+        means = None
+        for begin in range(0, local, CHUNK):
+            power = jnp.dot(
+                left, train_aug[:, begin : begin + CHUNK], preferred_element_type=jnp.float32
+            )
+            values = jnp.exp2(power * LOG2E).astype(jnp.bfloat16)
+            scaled = values.astype(jnp.float32) * wide[:, begin : begin + CHUNK]
+            for lane in range(0, CHUNK, 128):
+                piece = scaled[:, lane : lane + 128]
+                means = piece if means is None else means + piece
+            product = jnp.dot(
+                values, factor_ref[begin : begin + CHUNK, :], preferred_element_type=jnp.float32
+            )
+            total = product if total is None else total + product
+        part[step] = total
+        for index, at in enumerate(where):
+            mean_acc[pl.ds(at, group), :] = means[index * group : (index + 1) * group, :]
+
+    def send(source, target, ssem, rsem, device):
+        return pltpu.make_async_remote_copy(
+            src_ref=source, dst_ref=target, send_sem=ssem, recv_sem=rsem, device_id={"trn": device}
+        )
+
+    def copy_y(s):
+        return send(part.at[s, 4 * group : 6 * group], got_y.at[s], s_y.at[s], r_y.at[s], other)
+
+    def first_b(s, got, begin, ssem, rsem, device):
+        return send(part.at[s, begin : begin + 2 * group], got.at[s], ssem.at[s], rsem.at[s], device)
+
+    def first_a(s, got, begin, ssem, rsem, device):
+        return send(part.at[s, begin : begin + group], got.at[s], ssem.at[s], rsem.at[s], device)
+
+    def onward(s, got, ssem, rsem, device):
+        return send(got.at[s], got.at[s], ssem.at[s], rsem.at[s], device)
+
+    def swap(s, got):
+        theirs = pl.ds(pl.multiple_of((1 - y) * group, group), group)
+        return send(got.at[s, theirs], got_x.at[s], s_x.at[s], r_x.at[s], other)
+
+    def square(values):
+        total = None
+        for lane in range(0, values.shape[1], 128):
+            piece = values[:, lane : lane + 128]
+            total = piece * piece if total is None else total + piece * piece
+        return total
+
+    chains_b = (
+        (got_br, 0, s_br, r_br, z, up, LAG_B),
+        (got_bl, 2 * group, s_bl, r_bl, last - z, down, LAG_B),
+    )
+    chains_a = (
+        (got_ar, 7 * group, s_ar, r_ar, z, up, LAG_A),
+        (got_al, 6 * group, s_al, r_al, last - z, down, LAG_A),
+    )
+
+    def lag_of(hop, table):
+        value = table[1]
+        for index in range(2, LINE):
+            value = jnp.where(hop == index, table[index], value)
+        return value
+
+    def inside(s):
+        return (s >= 0) & (s < STEPS)
+
+    compute(0)
+    pl.semaphore_wait(barrier, count - 1)
+
+    def turn(it, carry):
+        @pl.when((it > 0) & (it < STEPS))
+        def _():
+            compute(it)
+
+        @pl.when(it < STEPS)
+        def _():
+            copy_y(it).start()
+            for got, begin, ssem, rsem, hop, device, _ in chains_b:
+                @pl.when(hop == 0)
+                def _():
+                    first_b(it, got, begin, ssem, rsem, device).start()
+
+        for got, begin, ssem, rsem, hop, device, lags in chains_b:
+            s = it - lag_of(hop, lags)
+
+            @pl.when((hop > 0) & inside(s))
+            def _():
+                onward(s, got, ssem, rsem, device).wait_recv()
+                got[s] = got[s] + part[s, begin : begin + 2 * group]
+
+                @pl.when(hop < last)
+                def _():
+                    onward(s, got, ssem, rsem, device).start()
+
+                @pl.when(hop == last)
+                def _():
+                    swap(s, got).start()
+
+        s_here = it - LAG_Y
+
+        @pl.when(inside(s_here))
+        def _():
+            copy_y(s_here).wait_recv()
+            kept = slice(6 * group, 8 * group)
+            part[s_here, kept] = part[s_here, kept] + got_y[s_here]
+            for got, begin, ssem, rsem, hop, device, _ in chains_a:
+                @pl.when(hop == 0)
+                def _():
+                    first_a(s_here, got, begin, ssem, rsem, device).start()
+
+        for got, begin, ssem, rsem, hop, device, lags in chains_a:
+            s = it - lag_of(hop, lags)
+
+            @pl.when((hop > 0) & inside(s))
+            def _():
+                onward(s, got, ssem, rsem, device).wait_recv()
+
+                @pl.when(hop < last)
+                def _():
+                    got[s] = got[s] + part[s, begin : begin + group]
+                    onward(s, got, ssem, rsem, device).start()
+
+                @pl.when(hop == last)
+                def _():
+                    at = pl.multiple_of(span // 2 + s * group, group)
+                    var_acc[pl.ds(at, group), :] = square(got[s] + part[s, begin : begin + group])
+
+        s_last = it - LAG_X
+        for got, hop in ((got_br, z), (got_bl, last - z)):
+            @pl.when((hop == last) & inside(s_last))
+            def _():
+                swap(s_last, got).wait_recv()
+                mine = pl.ds(pl.multiple_of(y * group, group), group)
+                at = pl.multiple_of(s_last * group, group)
+                var_acc[pl.ds(at, group), :] = square(got[s_last, mine] + got_x[s_last])
+
+        @pl.when(it == STEPS)
+        def _():
+            for index in range(rows // 128):
+                block = mean_acc[index * 128 : (index + 1) * 128, :]
+                mean_box[me, index : index + 1, :] = jnp.sum(block.T, axis=0, keepdims=True)
+
+            def tell(k, carry):
+                mean_copy(k).start()
+                return carry
+
+            lax.fori_loop(1, count, tell, 0)
+
+        return carry
+
+    def mean_copy(k):
+        return send(
+            mean_box.at[me], mean_box.at[me], s_mean.at[k], r_mean.at[k], lax.rem(me + k, count)
+        )
+
+    lax.fori_loop(0, STEPS + LAG_X, turn, 0)
+
+    owner = jnp.where(z == last, 2, 0) + y
+    ends = (z == 0) | (z == last)
+
+    def var_copy(k, who):
+        return send(var_box.at[who], var_box.at[who], s_var.at[k], r_var.at[who], lax.rem(me + k, count))
+
+    @pl.when(ends)
+    def _():
+        for index in range(span // 128):
+            block = var_acc[index * 128 : (index + 1) * 128, :]
+            var_box[owner, index : index + 1, :] = 1.0 - jnp.sum(block.T, axis=0, keepdims=True)
+
+        def tell(k, carry):
+            var_copy(k, owner).start()
+            return carry
+
+        lax.fori_loop(1, count, tell, 0)
+
+    def hear(k, carry):
+        mean_copy(k).wait()
+        return carry
+
+    lax.fori_loop(1, count, hear, 0)
+    total = mean_box[0]
+    for index in range(1, count):
+        total = total + mean_box[index]
+    mean_ref[...] = total
+
+    def settle(s, carry):
+        copy_y(s).wait_send()
+        for got, begin, ssem, rsem, hop, device, _ in chains_b:
+            @pl.when(hop == 0)
+            def _():
+                first_b(s, got, begin, ssem, rsem, device).wait_send()
+
+            @pl.when((hop > 0) & (hop < last))
+            def _():
+                onward(s, got, ssem, rsem, device).wait_send()
+
+            @pl.when(hop == last)
+            def _():
+                swap(s, got).wait_send()
+
+        for got, begin, ssem, rsem, hop, device, _ in chains_a:
+            @pl.when(hop == 0)
+            def _():
+                first_a(s, got, begin, ssem, rsem, device).wait_send()
+
+            @pl.when((hop > 0) & (hop < last))
+            def _():
+                onward(s, got, ssem, rsem, device).wait_send()
+
+        return carry
+
+    lax.fori_loop(0, STEPS, settle, 0)
+
+    for who in range(4):
+        @pl.when(jnp.logical_not(ends) | (owner != who))
+        def _():
+            var_copy(1, who).wait_recv()
+
+    lines = span // 128
+    for who in range(4):
+        var_ref[who * lines : (who + 1) * lines, :] = var_box[who]
+
+    @pl.when(ends)
+    def _():
+        def done(k, carry):
+            var_copy(k, owner).wait_send()
+            return carry
+
+        lax.fori_loop(1, count, done, 0)
+
+
+def fused(test_points, train_points, weights, factor, *, count):
+    dim, rows = test_points.shape
+    local = train_points.shape[1]
+    width = factor.shape[1]
+    depth = -(-(dim + 16) // 128) * 128
+    group = rows // (8 * STEPS)
+    dma = pltpu.SemaphoreType.DMA
+    f32 = jnp.float32
+    sems = [dma((STEPS,))] * 12 + [dma((count,)), dma((count,)), dma((count,)), dma((4,))]
+    mean, variance = pl.pallas_call(
+        kernel,
+        out_shape=[jax.ShapeDtypeStruct((rows // 128, 128), f32)] * 2,
+        in_specs=[pl.BlockSpec(memory_space=pltpu.VMEM)] * 4,
+        out_specs=[pl.BlockSpec(memory_space=pltpu.VMEM)] * 2,
+        scratch_shapes=[
+            pltpu.VMEM((rows, depth), jnp.bfloat16),
+            pltpu.VMEM((depth, local), jnp.bfloat16),
+            pltpu.VMEM((1, local), f32),
+            pltpu.VMEM((STEPS, 8 * group, width), f32),
+            pltpu.VMEM((STEPS, 2 * group, width), f32),
+            pltpu.VMEM((STEPS, 2 * group, width), f32),
+            pltpu.VMEM((STEPS, 2 * group, width), f32),
+            pltpu.VMEM((STEPS, group, width), f32),
+            pltpu.VMEM((STEPS, group, width), f32),
+            pltpu.VMEM((STEPS, group, width), f32),
+            pltpu.VMEM((rows, 128), f32),
+            pltpu.VMEM((rows // 4, 128), f32),
+            pltpu.VMEM((count, rows // 128, 128), f32),
+            pltpu.VMEM((4, rows // 512, 128), f32),
+        ] + sems,
+        compiler_params=pltpu.CompilerParams(
+            collective_id=0, has_side_effects=True, vmem_limit_bytes=56 * 1024 * 1024
+        ),
+    )(test_points, train_points, weights.reshape(1, local), factor)
+    return mean.reshape(rows), variance.reshape(rows)
 
 
 def on_device(test_points, train_points, weights, factor):
@@ -54,6 +422,8 @@
         P(("grp", "trn"), None),
     )
     out_specs = (P(("grp", "tst")), P(("grp", "tst")))
+    count = mesh.shape["trn"]
+    body = functools.partial(fused, count=count) if count == 2 * LINE else on_device
     return jax.shard_map(
-        on_device, mesh=mesh, in_specs=in_specs, out_specs=out_specs, check_vma=False
-    )
+        body, mesh=mesh, in_specs=in_specs, out_specs=out_specs, check_vma=False
+    )

time: 190 us -> 71.1 us (0.37)
  Pallas kernels: 0 us -> 66.2 us
  blocking collectives: 60.9 us -> 0 us
  matrix products: 54.4 us -> 0 us
  waiting for transfers between devices: 48.5 us -> 0 us
  between operations: 14.7 us -> 0.64 us
  other arithmetic: 6.01 us -> 0 us
    pallas_call x0 -> x1, Pallas kernels: none -> 66.2 us  [fused(): pl.pallas_call(kernel, out_shape=[jax.ShapeDtypeStruct((rows // 128, 128)...]
    dot_general x12 -> x0, matrix products: 54.4 us -> none  [the longest x4 31.8 us: step(): jnp.dot(kernel, fblock, preferred_element_type=jnp.float32)]
    reduce_scatter x1 -> x0, waiting for transfers between devices: 48.5 us -> none  [on_device(): lax.psum_scatter(proj_part, 'trn', scatter_dimension=0, tiled=True)]
    all_gather x2 -> x0, blocking collectives: 36.3 us -> none  [the longest x1 19.2 us: on_device(): lax.all_gather(var_share, 'trn', axis=0, tiled=True)]
    unnamed x1 -> x0, blocking collectives: 24.6 us -> none
    reduce_sum x6 -> x0, other arithmetic: 5.97 us -> none  [the longest x4 3.79 us: step(): train_sq = jnp.sum(points.astype(jnp.float32) ** 2, axis=0)]
    dynamic_slice x8 -> x0, local copies, waits for them, and re-layouts: 2.76 us -> none  [step(): wblock = lax.dynamic_slice_in_dim(weights, start, block, 0)]
  transfers between devices with their start and end apart: 1 -> 0, of which waited for: 1 -> 0; matrix products, arithmetic and copies ran while one was open for 0% -> 0% of each run, Pallas kernels for 0% -> 0%
where the time goes in v1:
time: 71.1 us; the launch traced here: 70.8 us
  Pallas kernels  66.2 us (93%)
  local copies, waits for them, and re-layouts  3.9 us (5%)
    pallas_call x1, Pallas kernels, fused(): pl.pallas_call(kernel, out_shape=[jax.ShapeDtypeStruct((rows // 128, 128)...  66.2 us
    unnamed x2, local copies, waits for them, and re-layouts  2.59 us

profile of v1, /device:TPU:0, one launch (start us, length us, event | category | flops | bytes accessed | tf_op | source)
XLA Modules:
  0.0 70.8 jit_solution(13565213015052587499)
XLA Ops:
  0.6 1.3 %reshape.13.weights_ref = bf16[1,4096]{1,0:T(2,128)(2,1)} reshape(bf16[4096]{0:T(1024)(128)(2,1)} %param.6) | data formatting | bytes 16384 | tf_op jit(solution)/shard_map/reshape | solution.py:373
  1.9 66.2 %shard_map.59 = (f32[16,128]{1,0:T(8,128)}, f32[16,128]{1,0:T(8,128)}) custom-call(bf16[64,2048]{1,0:T(8,128)(2,1)} %test_ref.1, bf16[64,4096]{1,0:T(8,128)(2,1)} %train_ref.1, bf16[1,4096]{1,0:T(2,128)(2,1)} %reshape.13.weights_ref, bf16[4096,512]{1,0:T(8,128)(2,1)} %factor_ref.1), custom_call_target="tpu_custom_call" | custom-call | tf_op jit(solution)/shard_map/pallas_call | solution.py:349
  68.2 1.3 %copy.8 = f32[2048]{0:T(1024)} copy(f32[2048]{0:T(1024)} %bitcast.3) | data formatting | bytes 16384
  69.5 1.3 %copy.9 = f32[2048]{0:T(1024)} copy(f32[2048]{0:T(1024)} %bitcast.2) | data formatting | bytes 16384

commit v2 on v1

--- a/solution.py
+++ b/solution.py
@@ -9,13 +9,14 @@
 from jax.sharding import PartitionSpec as P
 
 LOG2E = 1.4426950408889634
-STEPS = 8
+STEPS = 16
+SHARE = 4
 CHUNK = 1024
 LINE = 4
 LAG_Y = 3
 LAG_B = (0, 3, 5, 7)
-LAG_A = (0, 5, 7, 9)
-LAG_X = 10
+LAG_A = (0, 7, 9, 11)
+LAG_X = 11
 
 
 def pieces(value):
@@ -34,11 +35,11 @@
 
 
 def kernel(
-    test_ref, train_ref, weights_ref, factor_ref, mean_ref, var_ref,
+    test_ref, train_ref, weights_ref, factor_hbm, mean_ref, var_ref,
     test_aug, train_aug, wide, part, got_y, got_br, got_bl, got_ar, got_al, got_x,
     mean_acc, var_acc, mean_box, var_box,
     s_y, r_y, s_br, r_br, s_bl, r_bl, s_ar, r_ar, s_al, r_al, s_x, r_x,
-    s_mean, r_mean, s_var, r_var,
+    s_mean, r_mean, s_var, r_var, factor_ref, factor_sem,
 ):
     count = mean_box.shape[0]
     pair = count // LINE
@@ -49,18 +50,24 @@
     dim, rows = test_ref.shape
     local = train_ref.shape[1]
     depth = test_aug.shape[1]
-    group = rows // (8 * STEPS)
+    quarter = rows // (4 * STEPS)
+    gb = quarter * SHARE // 8
+    ga = quarter - gb
     span = rows // 4
     other = z * pair + (1 - y)
     up, down = me + pair, me - pair
 
     barrier = pltpu.get_barrier_semaphore()
 
-    def greet(k, carry):
-        pl.semaphore_signal(barrier, inc=1, device_id={"trn": lax.rem(me + k, count)})
-        return carry
-
-    lax.fori_loop(1, count, greet, 0)
+    def greet(device):
+        pl.semaphore_signal(barrier, inc=1, device_id={"trn": device})
+
+    greet(other)
+    pl.when(z < last)(lambda: greet(up))
+    pl.when(z > 0)(lambda: greet(down))
+
+    fetch = pltpu.make_async_copy(factor_hbm, factor_ref, factor_sem)
+    fetch.start()
 
     def prepare_train(index, carry):
         cols = pl.ds(pl.multiple_of(index * 512, 512), 512)
@@ -90,13 +97,14 @@
         whole = jnp.concatenate(
             [points * (8.0 / dim), extra, jnp.zeros((depth - dim - 8, 256), jnp.float32)], axis=0
         )
-        test_aug[cols, :] = whole.T.astype(jnp.bfloat16)
+        test_aug[cols, :] = whole.T
         return carry
 
     lax.fori_loop(0, rows // 256, prepare_test, 0)
 
     def row_of(owner, kind, step):
-        return pl.multiple_of(owner * span + kind * (span // 2) + step * group, group)
+        inner = gb * STEPS + step * ga if kind else step * gb
+        return pl.multiple_of(owner * span + inner, 8)
 
     def places(step):
         return (
@@ -106,7 +114,10 @@
 
     def compute(step):
         where = places(step)
-        left = jnp.concatenate([test_aug[pl.ds(at, group), :] for at in where], axis=0)
+        sizes = (gb,) * 4 + (ga,) * 4
+        left = jnp.concatenate(
+            [test_aug[pl.ds(at, size), :] for at, size in zip(where, sizes)], axis=0
+        ).astype(jnp.bfloat16)
         total = None
         means = None
         for begin in range(0, local, CHUNK):
@@ -123,8 +134,10 @@
             )
             total = product if total is None else total + product
         part[step] = total
-        for index, at in enumerate(where):
-            mean_acc[pl.ds(at, group), :] = means[index * group : (index + 1) * group, :]
+        begin = 0
+        for at, size in zip(where, sizes):
+            mean_acc[pl.ds(at, size), :] = means[begin : begin + size, :]
+            begin += size
 
     def send(source, target, ssem, rsem, device):
         return pltpu.make_async_remote_copy(
@@ -132,19 +145,19 @@
         )
 
     def copy_y(s):
-        return send(part.at[s, 4 * group : 6 * group], got_y.at[s], s_y.at[s], r_y.at[s], other)
+        return send(part.at[s, 4 * gb : 4 * gb + 2 * ga], got_y.at[s], s_y.at[s], r_y.at[s], other)
 
     def first_b(s, got, begin, ssem, rsem, device):
-        return send(part.at[s, begin : begin + 2 * group], got.at[s], ssem.at[s], rsem.at[s], device)
+        return send(part.at[s, begin : begin + 2 * gb], got.at[s], ssem.at[s], rsem.at[s], device)
 
     def first_a(s, got, begin, ssem, rsem, device):
-        return send(part.at[s, begin : begin + group], got.at[s], ssem.at[s], rsem.at[s], device)
+        return send(part.at[s, begin : begin + ga], got.at[s], ssem.at[s], rsem.at[s], device)
 
     def onward(s, got, ssem, rsem, device):
         return send(got.at[s], got.at[s], ssem.at[s], rsem.at[s], device)
 
     def swap(s, got):
-        theirs = pl.ds(pl.multiple_of((1 - y) * group, group), group)
+        theirs = pl.ds(pl.multiple_of((1 - y) * gb, 8), gb)
         return send(got.at[s, theirs], got_x.at[s], s_x.at[s], r_x.at[s], other)
 
     def square(values):
@@ -156,11 +169,11 @@
 
     chains_b = (
         (got_br, 0, s_br, r_br, z, up, LAG_B),
-        (got_bl, 2 * group, s_bl, r_bl, last - z, down, LAG_B),
+        (got_bl, 2 * gb, s_bl, r_bl, last - z, down, LAG_B),
     )
     chains_a = (
-        (got_ar, 7 * group, s_ar, r_ar, z, up, LAG_A),
-        (got_al, 6 * group, s_al, r_al, last - z, down, LAG_A),
+        (got_ar, 4 * gb + 3 * ga, s_ar, r_ar, z, up, LAG_A),
+        (got_al, 4 * gb + 2 * ga, s_al, r_al, last - z, down, LAG_A),
     )
 
     def lag_of(hop, table):
@@ -172,8 +185,12 @@
     def inside(s):
         return (s >= 0) & (s < STEPS)
 
+    fetch.wait()
     compute(0)
-    pl.semaphore_wait(barrier, count - 1)
+    between = (z > 0) & (z < last)
+    pl.when(between)(lambda: pl.semaphore_wait(barrier, 3))
+    pl.when(jnp.logical_not(between))(lambda: pl.semaphore_wait(barrier, 2))
+
 
     def turn(it, carry):
         @pl.when((it > 0) & (it < STEPS))
@@ -194,7 +211,7 @@
             @pl.when((hop > 0) & inside(s))
             def _():
                 onward(s, got, ssem, rsem, device).wait_recv()
-                got[s] = got[s] + part[s, begin : begin + 2 * group]
+                got[s] = got[s] + part[s, begin : begin + 2 * gb]
 
                 @pl.when(hop < last)
                 def _():
@@ -209,7 +226,7 @@
         @pl.when(inside(s_here))
         def _():
             copy_y(s_here).wait_recv()
-            kept = slice(6 * group, 8 * group)
+            kept = slice(4 * gb + 2 * ga, 4 * gb + 4 * ga)
             part[s_here, kept] = part[s_here, kept] + got_y[s_here]
             for got, begin, ssem, rsem, hop, device, _ in chains_a:
                 @pl.when(hop == 0)
@@ -225,24 +242,24 @@
 
                 @pl.when(hop < last)
                 def _():
-                    got[s] = got[s] + part[s, begin : begin + group]
+                    got[s] = got[s] + part[s, begin : begin + ga]
                     onward(s, got, ssem, rsem, device).start()
 
                 @pl.when(hop == last)
                 def _():
-                    at = pl.multiple_of(span // 2 + s * group, group)
-                    var_acc[pl.ds(at, group), :] = square(got[s] + part[s, begin : begin + group])
+                    at = pl.multiple_of(gb * STEPS + s * ga, 8)
+                    var_acc[pl.ds(at, ga), :] = square(got[s] + part[s, begin : begin + ga])
 
         s_last = it - LAG_X
         for got, hop in ((got_br, z), (got_bl, last - z)):
             @pl.when((hop == last) & inside(s_last))
             def _():
                 swap(s_last, got).wait_recv()
-                mine = pl.ds(pl.multiple_of(y * group, group), group)
-                at = pl.multiple_of(s_last * group, group)
-                var_acc[pl.ds(at, group), :] = square(got[s_last, mine] + got_x[s_last])
-
-        @pl.when(it == STEPS)
+                mine = pl.ds(pl.multiple_of(y * gb, 8), gb)
+                at = pl.multiple_of(s_last * gb, 8)
+                var_acc[pl.ds(at, gb), :] = square(got[s_last, mine] + got_x[s_last])
+
+        @pl.when(it == STEPS + LAG_Y)
         def _():
             for index in range(rows // 128):
                 block = mean_acc[index * 128 : (index + 1) * 128, :]
@@ -261,7 +278,7 @@
             mean_box.at[me], mean_box.at[me], s_mean.at[k], r_mean.at[k], lax.rem(me + k, count)
         )
 
-    lax.fori_loop(0, STEPS + LAG_X, turn, 0)
+    lax.fori_loop(0, STEPS + max(LAG_X, LAG_A[-1]), turn, 0)
 
     owner = jnp.where(z == last, 2, 0) + y
     ends = (z == 0) | (z == last)
@@ -342,31 +359,34 @@
     local = train_points.shape[1]
     width = factor.shape[1]
     depth = -(-(dim + 16) // 128) * 128
-    group = rows // (8 * STEPS)
+    quarter = rows // (4 * STEPS)
+    gb = quarter * SHARE // 8
+    ga = quarter - gb
     dma = pltpu.SemaphoreType.DMA
     f32 = jnp.float32
     sems = [dma((STEPS,))] * 12 + [dma((count,)), dma((count,)), dma((count,)), dma((4,))]
     mean, variance = pl.pallas_call(
         kernel,
         out_shape=[jax.ShapeDtypeStruct((rows // 128, 128), f32)] * 2,
-        in_specs=[pl.BlockSpec(memory_space=pltpu.VMEM)] * 4,
+        in_specs=[pl.BlockSpec(memory_space=pltpu.VMEM)] * 3
+        + [pl.BlockSpec(memory_space=pl.ANY)],
         out_specs=[pl.BlockSpec(memory_space=pltpu.VMEM)] * 2,
         scratch_shapes=[
-            pltpu.VMEM((rows, depth), jnp.bfloat16),
+            pltpu.VMEM((rows, depth), f32),
             pltpu.VMEM((depth, local), jnp.bfloat16),
             pltpu.VMEM((1, local), f32),
-            pltpu.VMEM((STEPS, 8 * group, width), f32),
-            pltpu.VMEM((STEPS, 2 * group, width), f32),
-            pltpu.VMEM((STEPS, 2 * group, width), f32),
-            pltpu.VMEM((STEPS, 2 * group, width), f32),
-            pltpu.VMEM((STEPS, group, width), f32),
-            pltpu.VMEM((STEPS, group, width), f32),
-            pltpu.VMEM((STEPS, group, width), f32),
+            pltpu.VMEM((STEPS, 4 * quarter, width), f32),
+            pltpu.VMEM((STEPS, 2 * ga, width), f32),
+            pltpu.VMEM((STEPS, 2 * gb, width), f32),
+            pltpu.VMEM((STEPS, 2 * gb, width), f32),
+            pltpu.VMEM((STEPS, ga, width), f32),
+            pltpu.VMEM((STEPS, ga, width), f32),
+            pltpu.VMEM((STEPS, gb, width), f32),
             pltpu.VMEM((rows, 128), f32),
             pltpu.VMEM((rows // 4, 128), f32),
             pltpu.VMEM((count, rows // 128, 128), f32),
             pltpu.VMEM((4, rows // 512, 128), f32),
-        ] + sems,
+        ] + sems + [pltpu.VMEM((local, width), jnp.bfloat16), dma],
         compiler_params=pltpu.CompilerParams(
             collective_id=0, has_side_effects=True, vmem_limit_bytes=56 * 1024 * 1024
         ),

time: 71.1 us -> 64.9 us (0.913)
  Pallas kernels: 66.2 us -> 60 us
    pallas_call x1, Pallas kernels: 66.2 us -> 60 us  [fused(): pl.pallas_call(kernel, out_shape=[jax.ShapeDtypeStruct((rows // 128, 128)...]
where the time goes in v2:
time: 64.9 us; the launch traced here: 64.6 us
  Pallas kernels  60 us (92%)
  local copies, waits for them, and re-layouts  3.9 us (6%)
    pallas_call x1, Pallas kernels, fused(): pl.pallas_call(kernel, out_shape=[jax.ShapeDtypeStruct((rows // 128, 128)...  60 us
    unnamed x2, local copies, waits for them, and re-layouts  2.59 us
    reshape x1, local copies, waits for them, and re-layouts, fused(): weights.reshape(1, local)  1.31 us

profile of v2, /device:TPU:0, one launch (start us, length us, event | category | flops | bytes accessed | tf_op | source)
XLA Modules:
  0.0 64.6 jit_solution(12855513162762968992)
XLA Ops:
  0.6 1.3 %reshape.13.weights_ref = bf16[1,4096]{1,0:T(2,128)(2,1)} reshape(bf16[4096]{0:T(1024)(128)(2,1)} %param.6) | data formatting | bytes 16384 | tf_op jit(solution)/shard_map/reshape | solution.py:393
  1.9 60.0 %shard_map.59 = (f32[16,128]{1,0:T(8,128)}, f32[16,128]{1,0:T(8,128)}) custom-call(bf16[64,2048]{1,0:T(8,128)(2,1)} %test_ref.1, bf16[64,4096]{1,0:T(8,128)(2,1)} %train_ref.1, bf16[1,4096]{1,0:T(2,128)(2,1)} %reshape.13.weights_ref, bf16[4096,512]{1,0:T(8,128)(2,1)} %factor_hbm.1), custom_call_target="tpu_custom_call" | custom-call | tf_op jit(solution)/shard_map/pallas_call | solution.py:368
  62.0 1.3 %copy.8 = f32[2048]{0:T(1024)} copy(f32[2048]{0:T(1024)} %bitcast.3) | data formatting | bytes 16384
  63.3 1.3 %copy.9 = f32[2048]{0:T(1024)} copy(f32[2048]{0:T(1024)} %bitcast.2) | data formatting | bytes 16384

commit v3 on v2

--- a/solution.py
+++ b/solution.py
@@ -35,7 +35,7 @@
 
 
 def kernel(
-    test_ref, train_ref, weights_ref, factor_hbm, mean_ref, var_ref,
+    test_ref, train_ref, weights_ref, factor_hbm, out_ref,
     test_aug, train_aug, wide, part, got_y, got_br, got_bl, got_ar, got_al, got_x,
     mean_acc, var_acc, mean_box, var_box,
     s_y, r_y, s_br, r_br, s_bl, r_bl, s_ar, r_ar, s_al, r_al, s_x, r_x,
@@ -306,7 +306,7 @@
     total = mean_box[0]
     for index in range(1, count):
         total = total + mean_box[index]
-    mean_ref[...] = total
+    out_ref[: rows // 128, :] = total
 
     def settle(s, carry):
         copy_y(s).wait_send()
@@ -343,7 +343,8 @@
 
     lines = span // 128
     for who in range(4):
-        var_ref[who * lines : (who + 1) * lines, :] = var_box[who]
+        begin = rows // 128 + who * lines
+        out_ref[begin : begin + lines, :] = var_box[who]
 
     @pl.when(ends)
     def _():
@@ -365,12 +366,12 @@
     dma = pltpu.SemaphoreType.DMA
     f32 = jnp.float32
     sems = [dma((STEPS,))] * 12 + [dma((count,)), dma((count,)), dma((count,)), dma((4,))]
-    mean, variance = pl.pallas_call(
+    out = pl.pallas_call(
         kernel,
-        out_shape=[jax.ShapeDtypeStruct((rows // 128, 128), f32)] * 2,
+        out_shape=jax.ShapeDtypeStruct((rows // 64, 128), f32),
         in_specs=[pl.BlockSpec(memory_space=pltpu.VMEM)] * 3
         + [pl.BlockSpec(memory_space=pl.ANY)],
-        out_specs=[pl.BlockSpec(memory_space=pltpu.VMEM)] * 2,
+        out_specs=pl.BlockSpec(memory_space=pltpu.VMEM),
         scratch_shapes=[
             pltpu.VMEM((rows, depth), f32),
             pltpu.VMEM((depth, local), jnp.bfloat16),
@@ -391,7 +392,8 @@
             collective_id=0, has_side_effects=True, vmem_limit_bytes=56 * 1024 * 1024
         ),
     )(test_points, train_points, weights.reshape(1, local), factor)
-    return mean.reshape(rows), variance.reshape(rows)
+    lines = rows // 128
+    return out[:lines].reshape(rows), out[lines:].reshape(rows)
 
 
 def on_device(test_points, train_points, weights, factor):

time: 64.9 us -> 63.5 us (0.978)
  local copies, waits for them, and re-layouts: 3.9 us -> 2.63 us
    unnamed x2 -> x0, local copies, waits for them, and re-layouts: 2.59 us -> none
    reshape x0 -> x1, local copies, waits for them, and re-layouts: none -> 1.32 us  [fused(): return (out[:lines].reshape(rows), out[lines:].reshape(rows))]
where the time goes in v3:
time: 63.5 us; the launch traced here: 63.3 us
  Pallas kernels  60 us (94%)
  local copies, waits for them, and re-layouts  2.63 us (4%)
  between operations  0.64 us (1%)
    pallas_call x1, Pallas kernels, fused(): pl.pallas_call(kernel, out_shape=jax.ShapeDtypeStruct((rows // 64, 128),...  60 us
    reshape x1, local copies, waits for them, and re-layouts, fused(): return (out[:lines].reshape(rows), out[lines:].reshape(rows))  1.32 us
    reshape x1, local copies, waits for them, and re-layouts, fused(): weights.reshape(1, local)  1.31 us

profile of v3, /device:TPU:0, one launch (start us, length us, event | category | flops | bytes accessed | tf_op | source)
XLA Modules:
  0.0 63.3 jit_solution(1846042984515975034)
XLA Ops:
  0.6 1.3 %reshape.13.weights_ref = bf16[1,4096]{1,0:T(2,128)(2,1)} reshape(bf16[4096]{0:T(1024)(128)(2,1)} %param.6) | data formatting | bytes 16384 | tf_op jit(solution)/shard_map/reshape | solution.py:394
  1.9 60.0 %shard_map.59 = f32[32,128]{1,0:T(8,128)} custom-call(bf16[64,2048]{1,0:T(8,128)(2,1)} %test_ref.1, bf16[64,4096]{1,0:T(8,128)(2,1)} %train_ref.1, bf16[1,4096]{1,0:T(2,128)(2,1)} %reshape.13.weights_ref, bf16[4096,512]{1,0:T(8,128)(2,1)} %factor_hbm.1), custom_call_target="tpu_custom_call" | custom-call | tf_op jit(solution)/shard_map/pallas_call | solution.py:369
  62.0 1.3 %slice_bitcast_fusion = (f32[2048]{0:T(1024)}, f32[2048]{0:T(1024)}) fusion(f32[32,128]{1,0:T(8,128)} %shard_map.59), kind=kLoop, calls=%fused_computation | loop fusion | bytes 32768 | tf_op jit(solution)/shard_map/reshape | solution.py:396
